TPU v7x, 32 devices: a whole 2x2x4 slice. The times are simulated.
32 devices in a mesh: span: 8 (over y, x, core), tok: 4 (over z).
Axes of the slice: x: 2, y: 2, z: 4, core: 2. Of those that a mesh axis runs over, the one named last changes fastest.
Arguments:
- queries: bfloat16 [8, 256, 3072], P('span', 'tok'), may hold values from -9 to 9
- keys: bfloat16 [8, 256, 3072], P('span', 'tok'), may hold values from -9 to 9
- values: bfloat16 [8, 256, 3072], P('span', 'tok'), may hold values from -6 to 6
- levels: int32 [8], P('span'), may hold values from 0 to 15
- retiring: int32 [1], replicated, may hold values from 0 to 7
- block_mask: int32 [8, 8], P('span'), may hold values 0 or 1
- gates: float32 [16, 3072], replicated, may hold values from 0.5 to 2
Outputs:
- attended: bfloat16 [8, 256, 3072], P('span', 'tok')
All inputs are finite; a program needn't handle non-finite values. No bound on the sum of `block_mask` on one device may be relied on, other than what follows from the above.
Results may differ from a plain program's by a relative error of at most 0.0085.
Values may be sent and summed in bfloat16 or wider, within the bound.
A program may use at most 128 MiB of HBM per device.

v0:
```python
import functools

import jax
import jax.numpy as jnp
from jax import lax
from jax.experimental import pallas as pl
from jax.experimental.pallas import tpu as pltpu
from jax.sharding import PartitionSpec as P

HEADS = 24
HEAD_DIM = 128
QUERY_BLOCK = 256
UNROLLED_KEYS = 2048


def ORDER(hpd):
    return [(kind, h) for h in range(hpd) for kind in ("kv", "q")]


def WAITS(toks):
    return range(1, toks)


def kernel(dims, q_ref, k_ref, v_ref, mask_ref, level_ref, retiring_ref, gates_ref, out_ref,
           qbuf, kbuf, vbuf, maskb, levelb, retb, gateb, mbuf, sbuf, obuf, total,
           sent, got, got_q, meta_sem, fwd_sent, fwd_got, core_sent, core_got, out_sent, out_got):
    spans, toks, g, hpd, rows = dims
    chips = spans // 2
    groups = chips // g
    ctok = rows * toks
    d = HEAD_DIM
    s = lax.axis_index("span")
    t = lax.axis_index("tok")
    c = lax.rem(s, 2)
    p = lax.div(s, 2)
    j = lax.rem(p, g)
    hi = lax.div(p, g)
    own = hi * g
    other = 1 - c

    def span_of(hi_, j_, c_):
        return (hi_ * g + j_) * 2 + c_

    partners = [(dt, dj) for dt in range(toks) for dj in range(g) if (dt, dj) != (0, 0)]
    partners.sort(key=lambda a: a[0])

    def shift_tok(by):
        if toks & (toks - 1) == 0:
            low = 0
            bit = 1
            while bit < toks:
                mine_bit = lax.rem(lax.div(t, bit), 2)
                low = low + bit * (1 - mine_bit if by & bit else mine_bit)
                bit *= 2
            return low
        return lax.rem(t + by, toks)

    def partner(dt, dj):
        return shift_tok(dt), lax.rem(j + dj, g)

    barrier = pltpu.get_barrier_semaphore()
    count = 0
    for dt, dj in partners:
        t2, j2 = partner(dt, dj)
        pl.semaphore_signal(barrier, inc=1, device_id=(span_of(hi, j2, c), t2),
                            device_id_type=pl.DeviceIdType.MESH)
        count += 1
    for dh in range(1, groups):
        pl.semaphore_signal(barrier, inc=1, device_id=(span_of(lax.rem(hi + dh, groups), j, c), t),
                            device_id_type=pl.DeviceIdType.MESH)
        count += 1
    pl.semaphore_signal(barrier, inc=1, device_id=(span_of(hi, j, other), t),
                        device_id_type=pl.DeviceIdType.MESH)
    pl.semaphore_wait(barrier, count + 1)

    def cols(t_, j_, h):
        return pl.ds(pl.multiple_of(((t_ * g + j_) * hpd + h) * d, d), d)

    my_rows = pl.ds(pl.multiple_of(t * rows, rows), rows)

    near = [a for a in partners if a[0] == 0]
    far = [a for a in partners if a[0] != 0]

    def arrays(kind, h):
        if kind == "q":
            return ((q_ref, qbuf.at[h, j, my_rows]),), got_q.at[h]
        return ((k_ref, kbuf.at[h, c, p, my_rows]), (v_ref, vbuf.at[h, c, p, my_rows])), got.at[h, t]

    def issue(kind, h, which):
        pairs, arrive = arrays(kind, h)
        for dt, dj in which:
            t2, j2 = partner(dt, dj)
            for src, dst in pairs:
                pltpu.make_async_remote_copy(
                    src.at[:, cols(t2, j2, h)], dst, sent, arrive,
                    device_id=(span_of(hi, j2, c), t2), device_id_type=pl.DeviceIdType.MESH).start()

    def keep(kind, h):
        pairs, arrive = arrays(kind, h)
        for src, dst in pairs:
            pltpu.make_async_copy(src.at[:, cols(t, j, h)], dst, arrive).start()

    for h in range(hpd):
        keep("kv", h)
        issue("kv", h, near)
    for kind, h in (("kv", 0), ("q", 0))[:2 * hpd - 1]:
        issue(kind, h, far)
    for h in range(hpd):
        keep("q", h)
        issue("q", h, near)

    def wait_bytes(ref, sem):
        pltpu.make_async_copy(ref, ref, sem).wait()

    mine = pl.ds(pl.multiple_of((t * g + j) * hpd * d, d), hpd * d)
    pltpu.make_async_copy(retiring_ref, retb, meta_sem.at[2]).start()
    pltpu.make_async_copy(gates_ref.at[:, mine], gateb, meta_sem.at[3]).start()
    for n, (src, dst) in enumerate(((mask_ref, maskb.at[j]), (level_ref, levelb.at[j]))):
        pltpu.make_async_copy(src, dst, meta_sem.at[n]).start()
        for dj in range(1, g):
            t2, j2 = partner(0, dj)
            pltpu.make_async_remote_copy(
                src, dst, meta_sem.at[4 + n], meta_sem.at[n],
                device_id=(span_of(hi, j2, c), t2), device_id_type=pl.DeviceIdType.MESH).start()
    wait_bytes(retb, meta_sem.at[2])
    wait_bytes(gateb, meta_sem.at[3])
    wait_bytes(maskb, meta_sem.at[0])
    wait_bytes(levelb, meta_sem.at[1])
    lane = lax.broadcasted_iota(jnp.int32, (1, spans), 1)
    level_at = lax.broadcasted_iota(jnp.int32, gateb.shape, 0)

    def age(slot):
        return lax.rem(slot - retb[...] + spans, spans)

    for i in range(g):
        slot = span_of(hi, i, c)
        see = (lane == slot) | ((maskb[i] == 1) & (age(lane) < age(slot)))
        mbuf[i, 1:2, 0:spans] = jnp.where(see, 1.0, 0.0)
        mbuf[i, 0:1] = jnp.sum(jnp.where(level_at == levelb[i], gateb[...], 0.0), axis=0, keepdims=True)
    c2 = jnp.float32(HEAD_DIM ** -0.5 * 1.4426950408889634)
    unrolled = 2 * chips * ctok <= UNROLLED_KEYS
    block = min(QUERY_BLOCK, ctok)

    def loop(count, body, carry):
        if unrolled:
            for n in range(count):
                carry = body(n, carry)
            return carry
        return lax.fori_loop(0, count, body, carry)

    def seen(i, half, chip):
        flags = mbuf[i, 1:2, 0:spans]
        lane = lax.broadcasted_iota(jnp.int32, flags.shape, 1)
        hit = lane == chip * 2 + half
        return jnp.sum(jnp.where(hit, flags, 0.0), axis=1, keepdims=True) > 0.5

    def scores(h, i, at, half, slot0, top):
        query = qbuf[h, i, at]

        def body(chip, top):
            score = lax.dot_general(kbuf[h, half, chip], query, (((1,), (1,)), ((), ())),
                                    preferred_element_type=jnp.float32)
            sbuf[slot0 + chip] = score
            best = jnp.max(score, axis=0, keepdims=True)
            return jnp.maximum(top, jnp.where(seen(i, half, chip), best, -1e30))

        return loop(chips, body, top)

    def mix(h, i, half, slot0, shift, carry):
        def body(chip, carry):
            acc, norm = carry
            minus = jnp.where(seen(i, half, chip), shift, 1e30)
            weight = jnp.exp2(sbuf[slot0 + chip] * c2 - minus)
            norm = norm + jnp.sum(weight, axis=0, keepdims=True)
            acc = acc + lax.dot_general(vbuf[h, half, chip], weight.astype(jnp.bfloat16),
                                        (((0,), (0,)), ((), ())), preferred_element_type=jnp.float32)
            return acc, norm

        return loop(chips, body, carry)

    def unit(h, i, b):
        at = pl.ds(b * block, block)
        top = jnp.full((1, block), -1e30, jnp.float32)
        top = scores(h, i, at, c, 0, top)
        top = scores(h, i, at, other, chips, top)
        shift = top * c2
        carry = (jnp.zeros((d, block), jnp.float32), jnp.zeros((1, block), jnp.float32))
        carry = mix(h, i, c, 0, shift, carry)
        acc, norm = mix(h, i, other, chips, shift, carry)
        mixed = (acc / norm).T
        gate = mbuf[i, 0:1, pl.ds(pl.multiple_of(h * d, d), d)]
        obuf[h, i, at] = (mixed * gate).astype(jnp.bfloat16)

    def relay(h, t2):
        rows2 = pl.ds(pl.multiple_of(t2 * rows, rows), rows)
        wait_bytes(total.at[pl.ds(0, 2 * g * rows)], got.at[h, t2])
        for dh in range(1, groups):
            to = (span_of(lax.rem(hi + dh, groups), j, c), t)
            for n, buf in enumerate((kbuf, vbuf)):
                piece = buf.at[h, c, pl.ds(own, g), rows2]
                pltpu.make_async_remote_copy(
                    piece, piece, fwd_sent.at[h, n], fwd_got.at[h, n],
                    device_id=to, device_id_type=pl.DeviceIdType.MESH).start()

    for h in range(hpd):
        relay(h, t)

    def head(h, carry):
        for k in WAITS(toks):
            relay(h, shift_tok(k))
            if k == toks // 2 and h + 1 < hpd:
                issue("kv", h + 1, far)
                issue("q", h + 1, far)
        if groups > 1:
            for n, buf in enumerate((kbuf, vbuf)):
                wait_bytes(buf.at[h, c, pl.ds(0, (groups - 1) * g)], fwd_got.at[h, n])
        for n, buf in enumerate((kbuf, vbuf)):
            half = buf.at[h, c]
            pltpu.make_async_remote_copy(
                half, half, core_sent.at[h, n], core_got.at[h, n],
                device_id=(span_of(hi, j, other), t), device_id_type=pl.DeviceIdType.MESH).start()
        for n, buf in enumerate((kbuf, vbuf)):
            wait_bytes(buf.at[h, other], core_got.at[h, n])

        wait_bytes(qbuf.at[h], got_q.at[h])

        def one(i, carry):
            lax.fori_loop(0, ctok // block, lambda b, x: (unit(h, i, b), x)[1], 0)
            at = cols(t, j, h)
            for k in range(toks):
                t2 = lax.rem(t + toks // 2 + k, toks)
                piece = obuf.at[h, i, pl.ds(pl.multiple_of(t2 * rows, rows), rows)]
                to_self = (t2 == t) & (i == j)

                @pl.when(to_self)
                def _():
                    pltpu.make_async_copy(piece, out_ref.at[:, at], out_got).start()

                @pl.when(jnp.logical_not(to_self))
                def _():
                    pltpu.make_async_remote_copy(
                        piece, out_ref.at[:, at], out_sent, out_got,
                        device_id=(span_of(hi, i, c), t2), device_id_type=pl.DeviceIdType.MESH).start()
            return carry

        return lax.fori_loop(0, g, one, carry)

    for h in range(hpd):
        head(h, 0)
    wait_bytes(out_ref, out_got)
    wait_bytes(total.at[pl.ds(0, len(partners) * hpd * rows)], out_sent)
    wait_bytes(total.at[pl.ds(0, len(partners) * 3 * hpd * rows)], sent)
    if g > 1:
        wait_bytes(maskb.at[pl.ds(0, g - 1)], meta_sem.at[4])
        wait_bytes(levelb.at[pl.ds(0, g - 1)], meta_sem.at[5])
    for h in range(hpd):
        for n, buf in enumerate((kbuf, vbuf)):
            if groups > 1:
                wait_bytes(buf.at[h, c, pl.ds(0, (groups - 1) * g)], fwd_sent.at[h, n])
            wait_bytes(buf.at[h, c], core_sent.at[h, n])


def local(queries, keys, values, levels, retiring, block_mask, gates):
    rows = queries.shape[1]
    spans = lax.axis_size("span")
    toks = lax.axis_size("tok")
    per_tok = HEADS // toks
    g = 2 if per_tok % 2 == 0 and spans % 4 == 0 else 1
    hpd = per_tok // g
    chips = spans // 2
    ctok = rows * toks
    block = min(QUERY_BLOCK, ctok)
    feat = queries.shape[2]
    any_ = pl.BlockSpec(memory_space=pl.ANY)
    bf16, f32 = jnp.bfloat16, jnp.float32
    dma = pltpu.SemaphoreType.DMA
    out = pl.pallas_call(
        functools.partial(kernel, (spans, toks, g, hpd, rows)),
        out_shape=jax.ShapeDtypeStruct((rows, feat), bf16),
        in_specs=[any_] * 7,
        out_specs=pl.BlockSpec(memory_space=pltpu.VMEM),
        scratch_shapes=[
            pltpu.VMEM((hpd, g, ctok, HEAD_DIM), bf16),
            pltpu.VMEM((hpd, 2, chips, ctok, HEAD_DIM), bf16),
            pltpu.VMEM((hpd, 2, chips, ctok, HEAD_DIM), bf16),
            pltpu.VMEM((g, 1, spans), jnp.int32),
            pltpu.VMEM((g, 1, 1), jnp.int32),
            pltpu.VMEM((1, 1), jnp.int32),
            pltpu.VMEM((gates.shape[0], hpd * HEAD_DIM), f32),
            pltpu.VMEM((g, 8, hpd * HEAD_DIM), f32),
            pltpu.VMEM((2 * chips, ctok, block), f32),
            pltpu.VMEM((hpd, g, ctok, HEAD_DIM), bf16),
            pltpu.VMEM(((toks * g - 1) * 3 * hpd * rows, HEAD_DIM), bf16),
            dma, dma((hpd, toks)), dma((hpd,)), dma((6,)),
            dma((hpd, 2)), dma((hpd, 2)), dma((hpd, 2)), dma((hpd, 2)),
            dma, dma,
        ],
        compiler_params=pltpu.CompilerParams(
            collective_id=0, has_side_effects=True, vmem_limit_bytes=60 * 1024 * 1024),
    )(queries[0], keys[0], values[0], block_mask, levels[None], retiring[None], gates)
    return out[None]


def solution(mesh):
    return jax.shard_map(
        local,
        mesh=mesh,
        in_specs=(
            P("span", "tok", None),
            P("span", "tok", None),
            P("span", "tok", None),
            P("span"),
            P(),
            P("span", None),
            P(),
        ),
        out_specs=P("span", "tok", None),
        check_vma=False,
    )
```

profile of v0, /device:TPU:0, one launch (start us, length us, event | category | flops | bytes accessed | tf_op | source)
XLA Modules:
  0.0 50.9 jit_solution(13311191795982521606)
XLA Ops:
  1.3 47.8 %shard_map.73 = bf16[64,3072]{1,0:T(8,128)(2,1)} custom-call(bf16[64,3072]{1,0:T(8,128)(2,1)} %bitcast.9, bf16[64,3072]{1,0:T(8,128)(2,1)} %bitcast.10, bf16[64,3072]{1,0:T(8,128)(2,1)} %bitcast.11, s32[1,8]{1,0:T(1,128)} %mask_ref.1, s32[1,1]{1,0:T(1,128)} %bitcast.6.level_ref, s32[1,1]{1,0:T(1,128)} %bitcast.7.retiring_ref, f32[16,3072]{1,0:T(8,128)} %gates_ref.1), custom_call_target="tpu_custom_call" | custom-call | tf_op jit(solution)/shard_map/pallas_call | solution.py:277
  49.1 1.8 %copy.11 = bf16[1,64,3072]{2,1,0:T(8,128)(2,1)} copy(bf16[1,64,3072]{2,1,0:T(8,128)(2,1)} %bitcast.8) | data formatting | bytes 786432
where the time goes:
time: 51.1 us; the launch traced here: 50.9 us
  Pallas kernels  47.8 us (94%)
  local copies, waits for them, and re-layouts  1.77 us (3%)
  between operations  1.3 us (3%)
    pallas_call x1, Pallas kernels, local(): pl.pallas_call(functools.partial(kernel, (spans, toks, g, hpd, rows)), ou...  47.8 us
    unnamed x1, local copies, waits for them, and re-layouts  1.77 us

commit v1 on v0

--- a/solution.py
+++ b/solution.py
@@ -276,7 +276,7 @@
     dma = pltpu.SemaphoreType.DMA
     out = pl.pallas_call(
         functools.partial(kernel, (spans, toks, g, hpd, rows)),
-        out_shape=jax.ShapeDtypeStruct((rows, feat), bf16),
+        out_shape=pltpu.VMEM((rows, feat), bf16),
         in_specs=[any_] * 7,
         out_specs=pl.BlockSpec(memory_space=pltpu.VMEM),
         scratch_shapes=[
@@ -296,7 +296,7 @@
             dma, dma,
         ],
         compiler_params=pltpu.CompilerParams(
-            collective_id=0, has_side_effects=True, vmem_limit_bytes=60 * 1024 * 1024),
+            collective_id=0, has_side_effects=True, vmem_limit_bytes=60000000),
     )(queries[0], keys[0], values[0], block_mask, levels[None], retiring[None], gates)
     return out[None]
 

time: 51.1 us -> 49.3 us (0.965)
  local copies, waits for them, and re-layouts: 1.77 us -> 0.75 us
  Pallas kernels: 47.8 us -> 47.1 us
    unnamed x1, local copies, waits for them, and re-layouts: 1.77 us -> 0.75 us
    pallas_call x1, Pallas kernels: 47.8 us -> 47.1 us  [local(): pl.pallas_call(functools.partial(kernel, (spans, toks, g, hpd, rows)), ou...]
where the time goes in v1:
time: 49.3 us; the launch traced here: 49.1 us
  Pallas kernels  47.1 us (96%)
  between operations  1.3 us (3%)
  local copies, waits for them, and re-layouts  0.75 us (2%)
    pallas_call x1, Pallas kernels, local(): pl.pallas_call(functools.partial(kernel, (spans, toks, g, hpd, rows)), ou...  47.1 us

profile of v1, /device:TPU:0, one launch (start us, length us, event | category | flops | bytes accessed | tf_op | source)
XLA Modules:
  0.0 49.1 jit_solution(2997685693227975332)
XLA Ops:
  1.3 47.1 %shard_map.73 = bf16[64,3072]{1,0:T(8,128)(2,1)S(1)} custom-call(bf16[64,3072]{1,0:T(8,128)(2,1)} %bitcast.9, bf16[64,3072]{1,0:T(8,128)(2,1)} %bitcast.10, bf16[64,3072]{1,0:T(8,128)(2,1)} %bitcast.11, s32[1,8]{1,0:T(1,128)} %mask_ref.1, s32[1,1]{1,0:T(1,128)} %bitcast.6.level_ref, s32[1,1]{1,0:T(1,128)} %bitcast.7.retiring_ref, f32[16,3072]{1,0:T(8,128)} %gates_ref.1), custom_call_target="tpu_custom_call" | custom-call | tf_op jit(solution)/shard_map/pallas_call | solution.py:277
  48.4 0.7 %copy.9 = bf16[1,64,3072]{2,1,0:T(8,128)(2,1)} copy(bf16[1,64,3072]{2,1,0:T(8,128)(2,1)S(1)} %bitcast.8) | data formatting | bytes 786432

commit v2 on v1

--- a/solution.py
+++ b/solution.py
@@ -13,13 +13,39 @@
 UNROLLED_KEYS = 2048
 
 
-def ORDER(hpd):
-    return [(kind, h) for h in range(hpd) for kind in ("kv", "q")]
-
-
-def WAITS(toks):
-    return range(1, toks)
-
+def plan(hpd, toks, g):
+    half = toks // 2
+    cross, side, near, every = range(half, toks), range(1, half), (0,), range(toks)
+    steps = []
+    for h in range(hpd):
+        steps += [("keep", "kv", h), ("keep", "q", h)]
+    rest = [("kv", h) for h in range(1, hpd)] + [("q", h) for h in range(1, hpd)]
+    for kind in ("kv", "q"):
+        steps += [("send", kind, 0, cross), ("send", kind, 0, side), ("send", kind, 0, near)]
+    for kind, h in rest:
+        steps += [("inner", kind, h, cross), ("inner", kind, h, side), ("inner", kind, h, near)]
+    steps += ["meta"]
+    for k in range(toks):
+        steps += [("relay", 0, k)]
+        if k:
+            steps += [("swap", 0, k - 1)]
+    for kind, h in rest:
+        steps += [("outer", kind, h, cross), ("outer", kind, h, side), ("outer", kind, h, near)]
+    steps += [("relay", h, 0) for h in range(1, hpd)] + [("swap", h, 0) for h in range(1, hpd)]
+    steps += [("swap", 0, toks - 1), ("ready", 0), ("queried", 0)]
+    steps += [("mixed", 0, 0), ("give", 0, 0)]
+    for h in range(1, hpd):
+        for k in range(1, toks - 1):
+            steps += [("relay", h, k)]
+    for i in range(1, g):
+        steps += [("mixed", 0, i), ("give", 0, i)]
+    steps += [("relay", h, toks - 1) for h in range(1, hpd)]
+    for h in range(1, hpd):
+        steps += [("swap", h, k) for k in range(1, toks)]
+        steps += [("ready", h), ("queried", h)]
+        for i in range(g):
+            steps += [("mixed", h, i), ("give", h, i)]
+    return steps
 
 def kernel(dims, q_ref, k_ref, v_ref, mask_ref, level_ref, retiring_ref, gates_ref, out_ref,
            qbuf, kbuf, vbuf, maskb, levelb, retb, gateb, mbuf, sbuf, obuf, total,
@@ -41,22 +67,20 @@
     def span_of(hi_, j_, c_):
         return (hi_ * g + j_) * 2 + c_
 
-    partners = [(dt, dj) for dt in range(toks) for dj in range(g) if (dt, dj) != (0, 0)]
-    partners.sort(key=lambda a: a[0])
-
-    def shift_tok(by):
-        if toks & (toks - 1) == 0:
-            low = 0
-            bit = 1
-            while bit < toks:
-                mine_bit = lax.rem(lax.div(t, bit), 2)
-                low = low + bit * (1 - mine_bit if by & bit else mine_bit)
-                bit *= 2
-            return low
-        return lax.rem(t + by, toks)
-
-    def partner(dt, dj):
-        return shift_tok(dt), lax.rem(j + dj, g)
+    half = toks // 2
+
+    def place(k):
+        if toks % 2:
+            return lax.rem(t + k, toks)
+        side = lax.div(t, half)
+        if k < half:
+            return side * half + lax.rem(t + k, half)
+        return (1 - side) * (toks - 1 - (k - half)) + side * (k - half)
+
+    partners = [(k, dj) for k in range(toks) for dj in range(g) if (k, dj) != (0, 0)]
+
+    def partner(k, dj):
+        return place(k), lax.rem(j + dj, g)
 
     barrier = pltpu.get_barrier_semaphore()
     count = 0
@@ -78,9 +102,6 @@
 
     my_rows = pl.ds(pl.multiple_of(t * rows, rows), rows)
 
-    near = [a for a in partners if a[0] == 0]
-    far = [a for a in partners if a[0] != 0]
-
     def arrays(kind, h):
         if kind == "q":
             return ((q_ref, qbuf.at[h, j, my_rows]),), got_q.at[h]
@@ -100,14 +121,26 @@
         for src, dst in pairs:
             pltpu.make_async_copy(src.at[:, cols(t, j, h)], dst, arrive).start()
 
-    for h in range(hpd):
-        keep("kv", h)
-        issue("kv", h, near)
-    for kind, h in (("kv", 0), ("q", 0))[:2 * hpd - 1]:
-        issue(kind, h, far)
-    for h in range(hpd):
-        keep("q", h)
-        issue("q", h, near)
+    def send(kind, h, ks):
+        issue(kind, h, [a for a in partners if a[0] in ks])
+
+    outer = lax.rem(t + 1, toks) < 2 if toks > 2 else t >= 0
+
+    def send_outer(kind, h, ks):
+        @pl.when(outer)
+        def _():
+            send(kind, h, ks)
+
+    def send_inner(kind, h, ks):
+        @pl.when(jnp.logical_not(outer))
+        def _():
+            send(kind, h, ks)
+
+    sends = {"keep": keep, "send": send, "outer": send_outer, "inner": send_inner}
+    steps = plan(hpd, toks, g)
+    begin = steps.index("meta")
+    for step in steps[:begin]:
+        sends[step[0]](*step[1:])
 
     def wait_bytes(ref, sem):
         pltpu.make_async_copy(ref, ref, sem).wait()
@@ -191,62 +224,65 @@
         gate = mbuf[i, 0:1, pl.ds(pl.multiple_of(h * d, d), d)]
         obuf[h, i, at] = (mixed * gate).astype(jnp.bfloat16)
 
-    def relay(h, t2):
+    def forward(h, t2, first, many, to, sem, arrive):
         rows2 = pl.ds(pl.multiple_of(t2 * rows, rows), rows)
+        for buf in (kbuf, vbuf):
+            piece = buf.at[h, c, pl.ds(first, many), rows2]
+            pltpu.make_async_remote_copy(
+                piece, piece, sem, arrive, device_id=to, device_id_type=pl.DeviceIdType.MESH).start()
+
+    def relay(h, k):
+        t2 = place(k)
         wait_bytes(total.at[pl.ds(0, 2 * g * rows)], got.at[h, t2])
         for dh in range(1, groups):
-            to = (span_of(lax.rem(hi + dh, groups), j, c), t)
-            for n, buf in enumerate((kbuf, vbuf)):
-                piece = buf.at[h, c, pl.ds(own, g), rows2]
+            forward(h, t2, own, g, (span_of(lax.rem(hi + dh, groups), j, c), t), fwd_sent, fwd_got.at[h, t2])
+        forward(h, t2, own, g, (span_of(hi, j, other), t), core_sent, core_got.at[h])
+
+    def swap(h, k):
+        t2 = place(k)
+        if groups > 1:
+            wait_bytes(total.at[pl.ds(0, 2 * (groups - 1) * g * rows)], fwd_got.at[h, t2])
+        for dh in range(1, groups):
+            forward(h, t2, lax.rem(hi + dh, groups) * g, g, (span_of(hi, j, other), t), core_sent, core_got.at[h])
+
+    def ready(h):
+        both = pl.ds(0, 2)
+        wait_bytes(kbuf.at[h, both, pl.ds(0, chips)], core_got.at[h])
+
+    def queried(h):
+        wait_bytes(qbuf.at[h], got_q.at[h])
+
+    def mixed(h, i):
+        for b in range(ctok // block):
+            unit(h, i, b)
+
+    def give(h, i):
+        at = cols(t, j, h)
+        for k in reversed(range(toks)):
+            t2 = place(k)
+            piece = obuf.at[h, i, pl.ds(pl.multiple_of(t2 * rows, rows), rows)]
+
+            def remote():
                 pltpu.make_async_remote_copy(
-                    piece, piece, fwd_sent.at[h, n], fwd_got.at[h, n],
-                    device_id=to, device_id_type=pl.DeviceIdType.MESH).start()
-
-    for h in range(hpd):
-        relay(h, t)
-
-    def head(h, carry):
-        for k in WAITS(toks):
-            relay(h, shift_tok(k))
-            if k == toks // 2 and h + 1 < hpd:
-                issue("kv", h + 1, far)
-                issue("q", h + 1, far)
-        if groups > 1:
-            for n, buf in enumerate((kbuf, vbuf)):
-                wait_bytes(buf.at[h, c, pl.ds(0, (groups - 1) * g)], fwd_got.at[h, n])
-        for n, buf in enumerate((kbuf, vbuf)):
-            half = buf.at[h, c]
-            pltpu.make_async_remote_copy(
-                half, half, core_sent.at[h, n], core_got.at[h, n],
-                device_id=(span_of(hi, j, other), t), device_id_type=pl.DeviceIdType.MESH).start()
-        for n, buf in enumerate((kbuf, vbuf)):
-            wait_bytes(buf.at[h, other], core_got.at[h, n])
-
-        wait_bytes(qbuf.at[h], got_q.at[h])
-
-        def one(i, carry):
-            lax.fori_loop(0, ctok // block, lambda b, x: (unit(h, i, b), x)[1], 0)
-            at = cols(t, j, h)
-            for k in range(toks):
-                t2 = lax.rem(t + toks // 2 + k, toks)
-                piece = obuf.at[h, i, pl.ds(pl.multiple_of(t2 * rows, rows), rows)]
-                to_self = (t2 == t) & (i == j)
-
-                @pl.when(to_self)
-                def _():
-                    pltpu.make_async_copy(piece, out_ref.at[:, at], out_got).start()
-
-                @pl.when(jnp.logical_not(to_self))
-                def _():
-                    pltpu.make_async_remote_copy(
-                        piece, out_ref.at[:, at], out_sent, out_got,
-                        device_id=(span_of(hi, i, c), t2), device_id_type=pl.DeviceIdType.MESH).start()
-            return carry
-
-        return lax.fori_loop(0, g, one, carry)
-
-    for h in range(hpd):
-        head(h, 0)
+                    piece, out_ref.at[:, at], out_sent, out_got,
+                    device_id=(span_of(hi, i, c), t2), device_id_type=pl.DeviceIdType.MESH).start()
+
+            if k:
+                remote()
+                continue
+
+            @pl.when(i == j)
+            def _():
+                pltpu.make_async_copy(piece, out_ref.at[:, at], out_got).start()
+
+            @pl.when(i != j)
+            def _():
+                remote()
+
+    ops = {**sends, "relay": relay, "swap": swap, "ready": ready, "queried": queried,
+           "mixed": mixed, "give": give}
+    for step in steps[begin + 1:]:
+        ops[step[0]](*step[1:])
     wait_bytes(out_ref, out_got)
     wait_bytes(total.at[pl.ds(0, len(partners) * hpd * rows)], out_sent)
     wait_bytes(total.at[pl.ds(0, len(partners) * 3 * hpd * rows)], sent)
@@ -256,8 +292,8 @@
     for h in range(hpd):
         for n, buf in enumerate((kbuf, vbuf)):
             if groups > 1:
-                wait_bytes(buf.at[h, c, pl.ds(0, (groups - 1) * g)], fwd_sent.at[h, n])
-            wait_bytes(buf.at[h, c], core_sent.at[h, n])
+                wait_bytes(buf.at[h, c, pl.ds(0, (groups - 1) * g)], fwd_sent)
+            wait_bytes(buf.at[h, c], core_sent)
 
 
 def local(queries, keys, values, levels, retiring, block_mask, gates):
@@ -292,7 +328,7 @@
             pltpu.VMEM((hpd, g, ctok, HEAD_DIM), bf16),
             pltpu.VMEM(((toks * g - 1) * 3 * hpd * rows, HEAD_DIM), bf16),
             dma, dma((hpd, toks)), dma((hpd,)), dma((6,)),
-            dma((hpd, 2)), dma((hpd, 2)), dma((hpd, 2)), dma((hpd, 2)),
+            dma, dma((hpd, toks)), dma, dma((hpd,)),
             dma, dma,
         ],
         compiler_params=pltpu.CompilerParams(

time: 49.3 us -> 46.6 us (0.945)
  Pallas kernels: 47.1 us -> 44.2 us
    pallas_call x1, Pallas kernels: 47.1 us -> 44.2 us  [local(): pl.pallas_call(functools.partial(kernel, (spans, toks, g, hpd, rows)), ou...]
where the time goes in v2:
time: 46.6 us; the launch traced here: 46.3 us
  Pallas kernels  44.2 us (95%)
  between operations  1.3 us (3%)
  local copies, waits for them, and re-layouts  0.75 us (2%)
    pallas_call x1, Pallas kernels, local(): pl.pallas_call(functools.partial(kernel, (spans, toks, g, hpd, rows)), ou...  44.2 us

profile of v2, /device:TPU:0, one launch (start us, length us, event | category | flops | bytes accessed | tf_op | source)
XLA Modules:
  0.0 46.3 jit_solution(3117612766910709798)
XLA Ops:
  1.3 44.2 %shard_map.73 = bf16[64,3072]{1,0:T(8,128)(2,1)S(1)} custom-call(bf16[64,3072]{1,0:T(8,128)(2,1)} %bitcast.9, bf16[64,3072]{1,0:T(8,128)(2,1)} %bitcast.10, bf16[64,3072]{1,0:T(8,128)(2,1)} %bitcast.11, s32[1,8]{1,0:T(1,128)} %mask_ref.1, s32[1,1]{1,0:T(1,128)} %bitcast.6.level_ref, s32[1,1]{1,0:T(1,128)} %bitcast.7.retiring_ref, f32[16,3072]{1,0:T(8,128)} %gates_ref.1), custom_call_target="tpu_custom_call" | custom-call | tf_op jit(solution)/shard_map/pallas_call | solution.py:313
  45.5 0.7 %copy.9 = bf16[1,64,3072]{2,1,0:T(8,128)(2,1)} copy(bf16[1,64,3072]{2,1,0:T(8,128)(2,1)S(1)} %bitcast.8) | data formatting | bytes 786432

commit v3 on v2

--- a/solution.py
+++ b/solution.py
@@ -19,30 +19,24 @@
     steps = []
     for h in range(hpd):
         steps += [("keep", "kv", h), ("keep", "q", h)]
-    rest = [("kv", h) for h in range(1, hpd)] + [("q", h) for h in range(1, hpd)]
-    for kind in ("kv", "q"):
-        steps += [("send", kind, 0, cross), ("send", kind, 0, side), ("send", kind, 0, near)]
-    for kind, h in rest:
-        steps += [("inner", kind, h, cross), ("inner", kind, h, side), ("inner", kind, h, near)]
+    kinds = [("kv", h) for h in range(hpd)]
+    qs = [("q", h) for h in range(hpd)]
+    for kind in kinds:
+        steps += [("send", *kind, part) for part in (cross, side, near)]
+    for kind in qs:
+        steps += [("inner", *kind, part) for part in (cross, side, near)]
     steps += ["meta"]
-    for k in range(toks):
-        steps += [("relay", 0, k)]
-        if k:
-            steps += [("swap", 0, k - 1)]
-    for kind, h in rest:
-        steps += [("outer", kind, h, cross), ("outer", kind, h, side), ("outer", kind, h, near)]
-    steps += [("relay", h, 0) for h in range(1, hpd)] + [("swap", h, 0) for h in range(1, hpd)]
-    steps += [("swap", 0, toks - 1), ("ready", 0), ("queried", 0)]
-    steps += [("mixed", 0, 0), ("give", 0, 0)]
-    for h in range(1, hpd):
-        for k in range(1, toks - 1):
-            steps += [("relay", h, k)]
-    for i in range(1, g):
-        steps += [("mixed", 0, i), ("give", 0, i)]
-    steps += [("relay", h, toks - 1) for h in range(1, hpd)]
-    for h in range(1, hpd):
-        steps += [("swap", h, k) for k in range(1, toks)]
-        steps += [("ready", h), ("queried", h)]
+    arrivals = [(h, 0) for h in range(hpd)] + [(h, k) for h in range(hpd) for k in range(1, toks)]
+    lag, pending = 3, []
+    for n, (h, k) in enumerate(arrivals):
+        steps += [("relay", h, k)]
+        pending += [(h, k)]
+        if len(pending) > lag:
+            steps += [("swap", *pending.pop(0))]
+        if (h, k) == (hpd - 1, toks - 1):
+            steps += [("outer", *kind, part) for kind in qs for part in (cross, side, near)]
+    for h in range(hpd):
+        steps += [("swap", *a) for a in pending if a[0] == h] + [("ready", h), ("queried", h)]
         for i in range(g):
             steps += [("mixed", h, i), ("give", h, i)]
     return steps

time: 46.6 us -> 43.8 us (0.940)
  Pallas kernels: 44.2 us -> 41.2 us
    pallas_call x1, Pallas kernels: 44.2 us -> 41.2 us  [local(): pl.pallas_call(functools.partial(kernel, (spans, toks, g, hpd, rows)), ou...]
where the time goes in v3:
time: 43.8 us; the launch traced here: 43.3 us
  Pallas kernels  41.2 us (94%)
  between operations  1.3 us (3%)
  local copies, waits for them, and re-layouts  0.75 us (2%)
    pallas_call x1, Pallas kernels, local(): pl.pallas_call(functools.partial(kernel, (spans, toks, g, hpd, rows)), ou...  41.2 us

profile of v3, /device:TPU:0, one launch (start us, length us, event | category | flops | bytes accessed | tf_op | source)
XLA Modules:
  0.0 43.3 jit_solution(15977306692898785476)
XLA Ops:
  1.3 41.2 %shard_map.73 = bf16[64,3072]{1,0:T(8,128)(2,1)S(1)} custom-call(bf16[64,3072]{1,0:T(8,128)(2,1)} %bitcast.9, bf16[64,3072]{1,0:T(8,128)(2,1)} %bitcast.10, bf16[64,3072]{1,0:T(8,128)(2,1)} %bitcast.11, s32[1,8]{1,0:T(1,128)} %mask_ref.1, s32[1,1]{1,0:T(1,128)} %bitcast.6.level_ref, s32[1,1]{1,0:T(1,128)} %bitcast.7.retiring_ref, f32[16,3072]{1,0:T(8,128)} %gates_ref.1), custom_call_target="tpu_custom_call" | custom-call | tf_op jit(solution)/shard_map/pallas_call | solution.py:307
  42.5 0.7 %copy.9 = bf16[1,64,3072]{2,1,0:T(8,128)(2,1)} copy(bf16[1,64,3072]{2,1,0:T(8,128)(2,1)S(1)} %bitcast.8) | data formatting | bytes 786432

commit v4 on v3

--- a/solution.py
+++ b/solution.py
@@ -26,7 +26,7 @@
     for kind in qs:
         steps += [("inner", *kind, part) for part in (cross, side, near)]
     steps += ["meta"]
-    arrivals = [(h, 0) for h in range(hpd)] + [(h, k) for h in range(hpd) for k in range(1, toks)]
+    arrivals = [(h, 0) for h in range(hpd)] + [(h, k) for h in range(hpd) for k in [*range(half, toks - 1), *range(1, half), toks - 1]]
     lag, pending = 3, []
     for n, (h, k) in enumerate(arrivals):
         steps += [("relay", h, k)]
@@ -252,7 +252,7 @@
 
     def give(h, i):
         at = cols(t, j, h)
-        for k in reversed(range(toks)):
+        for k in [*range(half, toks), *reversed(range(half))]:
             t2 = place(k)
             piece = obuf.at[h, i, pl.ds(pl.multiple_of(t2 * rows, rows), rows)]
 

time: 43.8 us -> 43.4 us (level)
  no operation moved by 1% of the time
where the time goes in v4:
time: 43.4 us; the launch traced here: 43.2 us
  Pallas kernels  41.2 us (95%)
  between operations  1.3 us (3%)
  local copies, waits for them, and re-layouts  0.75 us (2%)
    pallas_call x1, Pallas kernels, local(): pl.pallas_call(functools.partial(kernel, (spans, toks, g, hpd, rows)), ou...  41.2 us

profile of v4, /device:TPU:0, one launch (start us, length us, event | category | flops | bytes accessed | tf_op | source)
XLA Modules:
  0.0 43.2 jit_solution(14396320301702509303)
XLA Ops:
  1.3 41.2 %shard_map.73 = bf16[64,3072]{1,0:T(8,128)(2,1)S(1)} custom-call(bf16[64,3072]{1,0:T(8,128)(2,1)} %bitcast.9, bf16[64,3072]{1,0:T(8,128)(2,1)} %bitcast.10, bf16[64,3072]{1,0:T(8,128)(2,1)} %bitcast.11, s32[1,8]{1,0:T(1,128)} %mask_ref.1, s32[1,1]{1,0:T(1,128)} %bitcast.6.level_ref, s32[1,1]{1,0:T(1,128)} %bitcast.7.retiring_ref, f32[16,3072]{1,0:T(8,128)} %gates_ref.1), custom_call_target="tpu_custom_call" | custom-call | tf_op jit(solution)/shard_map/pallas_call | solution.py:307
  42.5 0.7 %copy.9 = bf16[1,64,3072]{2,1,0:T(8,128)(2,1)} copy(bf16[1,64,3072]{2,1,0:T(8,128)(2,1)S(1)} %bitcast.8) | data formatting | bytes 786432
